TPU v7x, 32 devices: a whole 2x2x4 slice. The times are simulated.
32 devices in a mesh: batch: 16 (over z, y, core), seq: 2 (over x).
Axes of the slice: x: 2, y: 2, z: 4, core: 2. Of those that a mesh axis runs over, the one named last changes fastest.
Arguments:
- queries: bfloat16 [4096, 4096], P(('batch', 'seq')), parts along dimension 0, may hold values from -130 to 130
- span_keys: bfloat16 [4096, 1024], P(('batch', 'seq')), parts along dimension 0, may hold values from -6 to 6
- span_values: bfloat16 [4096, 1024], P(('batch', 'seq')), parts along dimension 0, may hold values from -6 to 6
- cache_keys: bfloat16 [65536, 1024], P(('batch', 'seq')), parts along dimension 0, may hold values from -6 to 6
- cache_values: bfloat16 [65536, 1024], P(('batch', 'seq')), parts along dimension 0, may hold values from -6 to 6
- span_start: int32 [16], P('batch'), parts along dimension 0, may hold values from 2048 to 16383, as said below
- prompt_length: int32 [16], P('batch'), parts along dimension 0, may hold values from 2112 to 16639, as said below
- window_size: int32 [16], P('batch'), parts along dimension 0, may hold values from 2048 to 4096
Outputs:
- attended: bfloat16 [4096, 4096], P(('batch', 'seq')), parts along dimension 0
There are 16 independent parts, one for each index of `batch`. A program takes and returns all parts, laid end to end along the dimension named above; each array names one. Nothing has to cross between parts.
Inputs may be any that keep to these rules, and one draw needn't show every extreme that they name: Cache row j holds position span_start - 4096 + j and is unused where that is negative. `prompt_length`: lies between span_start + 64 and span_start + 256; block rows at or past it are padding.
All inputs are finite; a program needn't handle non-finite values.
Results may differ from a plain program's by a relative error of at most 0.0065.
Values may be sent and summed in bfloat16 or wider, within the bound.
A program may use at most 128 MiB of HBM per device.

v0:
```python
import functools

import jax
import jax.numpy as jnp
from jax import lax
from jax.experimental import pallas as pl
from jax.experimental.pallas import tpu as pltpu
from jax.sharding import PartitionSpec as P

HD = 128
NEG = -1e30
FLOOR = -1e29
LOG2E = 1.4426950408889634
MESH = pl.DeviceIdType.MESH


def chunks_of(total, size):
    return [(at, min(size, total - at)) for at in range(0, total, size)]


def kernel(
    n,
    start_hbm,
    length_hbm,
    window_hbm,
    q_hbm,
    sk_hbm,
    sv_hbm,
    ck_hbm,
    cv_hbm,
    out_ref,
    start_ref,
    length_ref,
    window_ref,
    q_own,
    q_got,
    keys,
    values,
    bias,
    scores,
    own_o,
    own_l,
    put_o,
    put_l,
    got_o,
    got_l,
    load_sem,
    own_sem,
    word_sem,
    qs_sem,
    qr_sem,
    os_sem,
    or_sem,
    ls_sem,
    lr_sem,
):
    me = lax.axis_index("seq")
    rows = q_hbm.shape[0]
    cached = ck_hbm.shape[0]
    span = sk_hbm.shape[0]
    total = cached + span
    heads = ck_hbm.shape[1] // HD
    groups = q_hbm.shape[1] // ck_hbm.shape[1]
    wide = groups * rows
    tile = 8 // groups
    factor = HD ** (-0.5) * LOG2E

    def kv_cols(h):
        return pl.ds(pl.multiple_of(h * HD, HD), HD)

    def q_cols(h):
        return pl.ds(pl.multiple_of(h * groups * HD, HD), groups * HD)

    def loads(h):
        return (
            pltpu.make_async_copy(
                ck_hbm.at[:, kv_cols(h)], keys.at[h, pl.ds(0, cached)], load_sem.at[h, 0]
            ),
            pltpu.make_async_copy(
                sk_hbm.at[:, kv_cols(h)], keys.at[h, pl.ds(cached, span)], load_sem.at[h, 1]
            ),
            pltpu.make_async_copy(
                cv_hbm.at[:, kv_cols(h)], values.at[h, pl.ds(0, cached)], load_sem.at[h, 2]
            ),
            pltpu.make_async_copy(
                sv_hbm.at[:, kv_cols(h)], values.at[h, pl.ds(cached, span)], load_sem.at[h, 3]
            ),
        )

    def ask(d, h):
        return pltpu.make_async_remote_copy(
            src_ref=q_own.at[h],
            dst_ref=q_got.at[d - 1, h],
            send_sem=qs_sem.at[d - 1, h],
            recv_sem=qr_sem.at[d - 1, h],
            device_id={"seq": lax.rem(me + d, n)},
            device_id_type=MESH,
        )

    def answer(d, h):
        return pltpu.make_async_remote_copy(
            src_ref=put_o.at[d - 1, h],
            dst_ref=got_o.at[d - 1, h],
            send_sem=os_sem.at[d - 1, h],
            recv_sem=or_sem.at[d - 1, h],
            device_id={"seq": lax.rem(me + n - d, n)},
            device_id_type=MESH,
        )

    def answer_l(d, t):
        return pltpu.make_async_remote_copy(
            src_ref=put_l.at[d - 1, t],
            dst_ref=got_l.at[d - 1, t],
            send_sem=ls_sem.at[d - 1, t],
            recv_sem=lr_sem.at[d - 1, t],
            device_id={"seq": lax.rem(me + n - d, n)},
            device_id_type=MESH,
        )

    barrier = pltpu.get_barrier_semaphore()
    for d in range(1, n):
        pl.semaphore_signal(
            barrier, inc=1, device_id={"seq": lax.rem(me + d, n)}, device_id_type=MESH
        )
    words = [
        pltpu.make_async_copy(src, dst, word_sem.at[i])
        for i, (src, dst) in enumerate(
            ((start_hbm, start_ref), (length_hbm, length_ref), (window_hbm, window_ref))
        )
    ]

    def own_copy(h):
        return pltpu.make_async_copy(q_hbm.at[:, q_cols(h)], q_own.at[h], own_sem.at[h])

    @pl.loop(0, heads)
    def _(h):
        own_copy(h).start()

    for copy in words:
        copy.start()
    for copy in loads(0):
        copy.start()
    if n > 1:
        pl.semaphore_wait(barrier, n - 1)

    @pl.loop(0, heads)
    def _(h):
        own_copy(h).wait()
        for d in range(1, n):
            ask(d, h).start()

    @pl.loop(1, heads)
    def _(h):
        for copy in loads(h):
            copy.start()

    for copy in words:
        copy.wait()
    start = start_ref[0]
    length = length_ref[0]
    window = window_ref[0]
    for d in range(n):
        source = lax.rem(me + n - d, n)
        q_pos = start + source * rows + lax.broadcasted_iota(jnp.int32, (1, rows), 1)
        high = jnp.where(q_pos < length, q_pos, -1)
        low = jnp.maximum(q_pos - window + 1, 0)
        for at, size in chunks_of(cached, 256):
            k_pos = (
                start
                + (me - n) * cached
                + at
                + lax.broadcasted_iota(jnp.int32, (size, rows), 0)
            )
            seen = (k_pos >= low) & (k_pos <= high)
            bias[d, pl.ds(at, size), :] = jnp.where(seen, 0.0, NEG).astype(jnp.bfloat16)
        k_pos = start + me * span + lax.broadcasted_iota(jnp.int32, (span, rows), 0)
        seen = (k_pos >= low) & (k_pos <= high)
        bias[d, pl.ds(cached, span), :] = jnp.where(seen, 0.0, NEG).astype(jnp.bfloat16)

    parts = chunks_of(cached, 256) + [(cached + at, size) for at, size in chunks_of(span, 256)]

    def unit(d, h, q):
        q_stack = jnp.concatenate(
            [q[:, g * HD : (g + 1) * HD] for g in range(groups)], axis=0
        )
        eye = (
            lax.broadcasted_iota(jnp.int32, (rows, rows), 0)
            == lax.broadcasted_iota(jnp.int32, (rows, rows), 1)
        )
        eye = jnp.where(eye, 1.0, 0.0).astype(jnp.bfloat16)
        q_wide = jnp.concatenate(
            [q_stack, jnp.concatenate([eye] * groups, axis=0)], axis=1
        )
        top = jnp.full((8, wide), FLOOR, jnp.float32)
        for at, size in parts:
            k_wide = jnp.concatenate(
                [keys[h, pl.ds(at, size), :], bias[d, pl.ds(at, size), :]], axis=1
            )
            s = lax.dot_general(
                k_wide, q_wide, (((1,), (1,)), ((), ())), preferred_element_type=jnp.float32
            )
            scores[pl.ds(at, size), :] = s
            top = jnp.maximum(top, jnp.max(s.reshape(size // 8, 8, wide), axis=0))
        top = jnp.max(top, axis=0, keepdims=True)
        sums = jnp.zeros((8, wide), jnp.float32)
        mixed = jnp.zeros((HD, wide), jnp.float32)
        for at, size in parts:
            w = jnp.exp2((scores[pl.ds(at, size), :] - top) * factor)
            sums = sums + jnp.sum(w.reshape(size // 8, 8, wide), axis=0)
            mixed = mixed + lax.dot_general(
                values[h, pl.ds(at, size), :],
                w.astype(jnp.bfloat16),
                (((0,), (0,)), ((), ())),
                preferred_element_type=jnp.float32,
            )
        sums = jnp.sum(sums, axis=0, keepdims=True)
        some = sums > 0.0
        safe = jnp.where(some, sums, 1.0)
        level = jnp.where(some, top * factor + jnp.log2(safe), NEG)
        return mixed / safe, level

    @pl.loop(0, heads)
    def _(h):
        for copy in loads(h):
            copy.wait()
        o, level = unit(0, h, q_own[h])
        own_o[h] = o
        for g in range(groups):
            own_l[h, pl.ds(g, 1), :] = level[:, g * rows : (g + 1) * rows]

        @pl.when(h > 0)
        def _():
            for d in range(1, n):
                answer(d, h - 1).start()

        for d in range(1, n):
            ask(d, h).wait_recv()
            o, level = unit(d, h, q_got[d - 1, h])
            put_o[d - 1, h] = o.astype(jnp.bfloat16)
            for g in range(groups):
                put_l[d - 1, h // tile, pl.ds(lax.rem(h, tile) * groups + g, 1), :] = level[
                    :, g * rows : (g + 1) * rows
                ]

        @pl.when(lax.rem(h, tile) == tile - 1)
        def _():
            for d in range(1, n):
                answer_l(d, h // tile).start()

    for d in range(1, n):
        answer(d, heads - 1).start()

    @pl.loop(0, heads)
    def _(h):
        @pl.when(lax.rem(h, tile) == 0)
        def _():
            for d in range(1, n):
                answer_l(d, h // tile).wait_recv()

        for d in range(1, n):
            answer(d, h).wait_recv()
        for g in range(groups):
            levels = [own_l[h, pl.ds(g, 1), :]] + [
                got_l[d - 1, h // tile, pl.ds(lax.rem(h, tile) * groups + g, 1), :]
                for d in range(1, n)
            ]
            best = functools.reduce(jnp.maximum, levels)
            shares = [jnp.exp2(level - best) for level in levels]
            across = pl.ds(g * rows, rows)
            o = own_o[h, :, across] * shares[0]
            for d in range(1, n):
                o = o + got_o[d - 1, h, :, across].astype(jnp.float32) * shares[d]
            o = o / functools.reduce(jnp.add, shares)
            cols = pl.ds(pl.multiple_of((h * groups + g) * HD, HD), HD)
            out_ref[:, cols] = o.T.astype(jnp.bfloat16)

    @pl.loop(0, heads)
    def _(h):
        for d in range(1, n):
            ask(d, h).wait_send()
            answer(d, h).wait_send()

    @pl.loop(0, heads // tile)
    def _(t):
        for d in range(1, n):
            answer_l(d, t).wait_send()


def body(n, queries, span_keys, span_values, cache_keys, cache_values, start, length, window):
    rows = queries.shape[0]
    cached = cache_keys.shape[0]
    span = span_keys.shape[0]
    total = cached + span
    heads = cache_keys.shape[1] // HD
    groups = queries.shape[1] // cache_keys.shape[1]
    wide = groups * rows
    peers = max(n - 1, 1)
    flops = 4 * n * queries.shape[1] * rows * total
    scratch = [
        pltpu.SMEM((1,), jnp.int32),
        pltpu.SMEM((1,), jnp.int32),
        pltpu.SMEM((1,), jnp.int32),
        pltpu.VMEM((heads, rows, groups * HD), jnp.bfloat16),
        pltpu.VMEM((peers, heads, rows, groups * HD), jnp.bfloat16),
        pltpu.VMEM((heads, total, HD), jnp.bfloat16),
        pltpu.VMEM((heads, total, HD), jnp.bfloat16),
        pltpu.VMEM((n, total, rows), jnp.bfloat16),
        pltpu.VMEM((total, wide), jnp.float32),
        pltpu.VMEM((heads, HD, wide), jnp.float32),
        pltpu.VMEM((heads, 8, rows), jnp.float32),
        pltpu.VMEM((peers, heads, HD, wide), jnp.bfloat16),
        pltpu.VMEM((peers, heads * groups // 8, 8, rows), jnp.float32),
        pltpu.VMEM((peers, heads, HD, wide), jnp.bfloat16),
        pltpu.VMEM((peers, heads * groups // 8, 8, rows), jnp.float32),
        pltpu.SemaphoreType.DMA((heads, 4)),
        pltpu.SemaphoreType.DMA((heads,)),
        pltpu.SemaphoreType.DMA((3,)),
        pltpu.SemaphoreType.DMA((peers, heads)),
        pltpu.SemaphoreType.DMA((peers, heads)),
        pltpu.SemaphoreType.DMA((peers, heads)),
        pltpu.SemaphoreType.DMA((peers, heads)),
        pltpu.SemaphoreType.DMA((peers, heads * groups // 8)),
        pltpu.SemaphoreType.DMA((peers, heads * groups // 8)),
    ]
    return pl.pallas_call(
        functools.partial(kernel, n),
        out_shape=pltpu.VMEM(queries.shape, jnp.bfloat16),
        in_specs=[pl.BlockSpec(memory_space=pltpu.HBM)] * 8,
        out_specs=pl.BlockSpec(memory_space=pltpu.VMEM),
        scratch_shapes=scratch,
        compiler_params=pltpu.CompilerParams(
            collective_id=0, has_side_effects=True, vmem_limit_bytes=56 * 1024 * 1024
        ),
        cost_estimate=pl.CostEstimate(
            flops=flops, bytes_accessed=4 * total * HD * heads, transcendentals=flops // (4 * HD)
        ),
        name="windowed",
    )(start, length, window, queries, span_keys, span_values, cache_keys, cache_values)


def solution(mesh):
    both = P(("batch", "seq"), None)
    placed = (both,) * 5 + (P("batch"),) * 3
    return jax.shard_map(
        functools.partial(body, mesh.shape["seq"]),
        mesh=mesh,
        in_specs=placed,
        out_specs=both,
        check_vma=False,
    )
```

profile of v0, /device:TPU:0, one launch (start us, length us, event | category | flops | bytes accessed | tf_op | source)
XLA Modules:
  0.0 53.8 jit_solution(8401370257807374016)
XLA Ops:
  1.9 50.8 %windowed.1 = bf16[128,4096]{1,0:T(8,128)(2,1)S(1)} custom-call(s32[1]{0:T(128)S(6)} %copy.11.start_hbm, s32[1]{0:T(128)S(6)} %copy.12.length_hbm, s32[1]{0:T(128)S(6)} %copy.13.window_hbm, bf16[128,4096]{1,0:T(8,128)(2,1)} %q_hbm.1, bf16[128,1024]{1,0:T(8,128)(2,1)} %sk_hbm.1, bf16[128,1024]{1,0:T(8,128)(2,1)} %sv_hbm.1, bf16[2048,1024]{1,0:T(8,128)(2,1)} %ck_hbm.1, ...), custom_call_target="tpu_custom_call" | custom-call | flops 9126805504 | bytes 8912896 | tf_op jit(solution)/shard_map/windowed/pallas_call | solution.py:325
  52.8 1.0 %copy.10 = bf16[128,4096]{1,0:T(8,128)(2,1)} copy(bf16[128,4096]{1,0:T(8,128)(2,1)S(1)} %windowed.1) | data formatting | bytes 2097152
where the time goes:
time: 53.9 us; the launch traced here: 53.8 us
  Pallas kernels  50.8 us (94%)
  between operations  1.95 us (4%)
  local copies, waits for them, and re-layouts  0.97 us (2%)
    pallas_call x1, Pallas kernels, body(): pl.pallas_call(functools.partial(kernel, n), out_shape=pltpu.VMEM(queries...  50.8 us

commit v1 on v0

--- a/solution.py
+++ b/solution.py
@@ -16,6 +16,23 @@
 
 def chunks_of(total, size):
     return [(at, min(size, total - at)) for at in range(0, total, size)]
+
+
+def grouped(sizes):
+    ends = [sum(sizes[: i + 1]) for i in range(len(sizes))]
+    return [(end - size, end) for size, end in zip(sizes, ends) if size > 0]
+
+
+def q_plan(heads):
+    return grouped([1, heads // 2 - 1, heads - heads // 2])
+
+
+def o_plan(heads):
+    return grouped([2] * ((heads - 2) // 2) + [1] * (heads - 2 * ((heads - 2) // 2)))
+
+
+def l_plan(tiles):
+    return grouped([tiles - 1, 1])
 
 
 def kernel(
@@ -87,32 +104,39 @@
             ),
         )
 
-    def ask(d, h):
+    asks = q_plan(heads)
+    answers = o_plan(heads)
+    tallies = l_plan(heads // tile)
+
+    def ask(d, i):
+        across = pl.ds(asks[i][0], asks[i][1] - asks[i][0])
         return pltpu.make_async_remote_copy(
-            src_ref=q_own.at[h],
-            dst_ref=q_got.at[d - 1, h],
-            send_sem=qs_sem.at[d - 1, h],
-            recv_sem=qr_sem.at[d - 1, h],
+            src_ref=q_own.at[across],
+            dst_ref=q_got.at[d - 1, across],
+            send_sem=qs_sem.at[d - 1, i],
+            recv_sem=qr_sem.at[d - 1, i],
             device_id={"seq": lax.rem(me + d, n)},
             device_id_type=MESH,
         )
 
-    def answer(d, h):
+    def answer(d, i):
+        across = pl.ds(answers[i][0], answers[i][1] - answers[i][0])
         return pltpu.make_async_remote_copy(
-            src_ref=put_o.at[d - 1, h],
-            dst_ref=got_o.at[d - 1, h],
-            send_sem=os_sem.at[d - 1, h],
-            recv_sem=or_sem.at[d - 1, h],
+            src_ref=put_o.at[d - 1, across],
+            dst_ref=got_o.at[d - 1, across],
+            send_sem=os_sem.at[d - 1, i],
+            recv_sem=or_sem.at[d - 1, i],
             device_id={"seq": lax.rem(me + n - d, n)},
             device_id_type=MESH,
         )
 
-    def answer_l(d, t):
+    def answer_l(d, i):
+        across = pl.ds(tallies[i][0], tallies[i][1] - tallies[i][0])
         return pltpu.make_async_remote_copy(
-            src_ref=put_l.at[d - 1, t],
-            dst_ref=got_l.at[d - 1, t],
-            send_sem=ls_sem.at[d - 1, t],
-            recv_sem=lr_sem.at[d - 1, t],
+            src_ref=put_l.at[d - 1, across],
+            dst_ref=got_l.at[d - 1, across],
+            send_sem=ls_sem.at[d - 1, i],
+            recv_sem=lr_sem.at[d - 1, i],
             device_id={"seq": lax.rem(me + n - d, n)},
             device_id_type=MESH,
         )
@@ -132,7 +156,16 @@
     def own_copy(h):
         return pltpu.make_async_copy(q_hbm.at[:, q_cols(h)], q_own.at[h], own_sem.at[h])
 
-    @pl.loop(0, heads)
+    for h in range(asks[0][1]):
+        own_copy(h).start()
+    if n > 1:
+        pl.semaphore_wait(barrier, n - 1)
+    for h in range(asks[0][1]):
+        own_copy(h).wait()
+    for d in range(1, n):
+        ask(d, 0).start()
+
+    @pl.loop(asks[0][1], heads)
     def _(h):
         own_copy(h).start()
 
@@ -140,14 +173,14 @@
         copy.start()
     for copy in loads(0):
         copy.start()
-    if n > 1:
-        pl.semaphore_wait(barrier, n - 1)
-
-    @pl.loop(0, heads)
-    def _(h):
-        own_copy(h).wait()
+    for i in range(1, len(asks)):
+
+        @pl.loop(asks[i][0], asks[i][1])
+        def _(h):
+            own_copy(h).wait()
+
         for d in range(1, n):
-            ask(d, h).start()
+            ask(d, i).start()
 
     @pl.loop(1, heads)
     def _(h):
@@ -228,13 +261,20 @@
         for g in range(groups):
             own_l[h, pl.ds(g, 1), :] = level[:, g * rows : (g + 1) * rows]
 
-        @pl.when(h > 0)
-        def _():
-            for d in range(1, n):
-                answer(d, h - 1).start()
+        for i, (_, end) in enumerate(answers[:-1]):
+
+            @pl.when(h == end)
+            def _(i=i):
+                for d in range(1, n):
+                    answer(d, i).start()
 
         for d in range(1, n):
-            ask(d, h).wait_recv()
+            for i, (first, _) in enumerate(asks):
+
+                @pl.when(h == first)
+                def _(d=d, i=i):
+                    ask(d, i).wait_recv()
+
             o, level = unit(d, h, q_got[d - 1, h])
             put_o[d - 1, h] = o.astype(jnp.bfloat16)
             for g in range(groups):
@@ -242,48 +282,48 @@
                     :, g * rows : (g + 1) * rows
                 ]
 
-        @pl.when(lax.rem(h, tile) == tile - 1)
-        def _():
-            for d in range(1, n):
-                answer_l(d, h // tile).start()
+        for i, (_, end) in enumerate(tallies):
+
+            @pl.when(h == end * tile - 1)
+            def _(i=i):
+                for d in range(1, n):
+                    answer_l(d, i).start()
 
     for d in range(1, n):
-        answer(d, heads - 1).start()
-
-    @pl.loop(0, heads)
-    def _(h):
-        @pl.when(lax.rem(h, tile) == 0)
-        def _():
-            for d in range(1, n):
-                answer_l(d, h // tile).wait_recv()
-
+        answer(d, len(answers) - 1).start()
+
+    for i, (first, last) in enumerate(answers):
+        for t, (at, _) in enumerate(tallies):
+            if first <= at * tile < last:
+                for d in range(1, n):
+                    answer_l(d, t).wait_recv()
         for d in range(1, n):
-            answer(d, h).wait_recv()
-        for g in range(groups):
-            levels = [own_l[h, pl.ds(g, 1), :]] + [
-                got_l[d - 1, h // tile, pl.ds(lax.rem(h, tile) * groups + g, 1), :]
-                for d in range(1, n)
-            ]
-            best = functools.reduce(jnp.maximum, levels)
-            shares = [jnp.exp2(level - best) for level in levels]
-            across = pl.ds(g * rows, rows)
-            o = own_o[h, :, across] * shares[0]
-            for d in range(1, n):
-                o = o + got_o[d - 1, h, :, across].astype(jnp.float32) * shares[d]
-            o = o / functools.reduce(jnp.add, shares)
-            cols = pl.ds(pl.multiple_of((h * groups + g) * HD, HD), HD)
-            out_ref[:, cols] = o.T.astype(jnp.bfloat16)
-
-    @pl.loop(0, heads)
-    def _(h):
-        for d in range(1, n):
-            ask(d, h).wait_send()
-            answer(d, h).wait_send()
-
-    @pl.loop(0, heads // tile)
-    def _(t):
-        for d in range(1, n):
-            answer_l(d, t).wait_send()
+            answer(d, i).wait_recv()
+
+        @pl.loop(first, last)
+        def _(h):
+            for g in range(groups):
+                levels = [own_l[h, pl.ds(g, 1), :]] + [
+                    got_l[d - 1, h // tile, pl.ds(lax.rem(h, tile) * groups + g, 1), :]
+                    for d in range(1, n)
+                ]
+                best = functools.reduce(jnp.maximum, levels)
+                shares = [jnp.exp2(level - best) for level in levels]
+                across = pl.ds(g * rows, rows)
+                o = own_o[h, :, across] * shares[0]
+                for d in range(1, n):
+                    o = o + got_o[d - 1, h, :, across].astype(jnp.float32) * shares[d]
+                o = o / functools.reduce(jnp.add, shares)
+                cols = pl.ds(pl.multiple_of((h * groups + g) * HD, HD), HD)
+                out_ref[:, cols] = o.T.astype(jnp.bfloat16)
+
+    for d in range(1, n):
+        for i in range(len(asks)):
+            ask(d, i).wait_send()
+        for i in range(len(answers)):
+            answer(d, i).wait_send()
+        for i in range(len(tallies)):
+            answer_l(d, i).wait_send()
 
 
 def body(n, queries, span_keys, span_values, cache_keys, cache_values, start, length, window):
@@ -315,12 +355,12 @@
         pltpu.SemaphoreType.DMA((heads, 4)),
         pltpu.SemaphoreType.DMA((heads,)),
         pltpu.SemaphoreType.DMA((3,)),
-        pltpu.SemaphoreType.DMA((peers, heads)),
-        pltpu.SemaphoreType.DMA((peers, heads)),
-        pltpu.SemaphoreType.DMA((peers, heads)),
-        pltpu.SemaphoreType.DMA((peers, heads)),
-        pltpu.SemaphoreType.DMA((peers, heads * groups // 8)),
-        pltpu.SemaphoreType.DMA((peers, heads * groups // 8)),
+        pltpu.SemaphoreType.DMA((peers, len(q_plan(heads)))),
+        pltpu.SemaphoreType.DMA((peers, len(q_plan(heads)))),
+        pltpu.SemaphoreType.DMA((peers, len(o_plan(heads)))),
+        pltpu.SemaphoreType.DMA((peers, len(o_plan(heads)))),
+        pltpu.SemaphoreType.DMA((peers, len(l_plan(heads * groups // 8)))),
+        pltpu.SemaphoreType.DMA((peers, len(l_plan(heads * groups // 8)))),
     ]
     return pl.pallas_call(
         functools.partial(kernel, n),

time: 53.9 us -> 53.7 us (level)
  no operation moved by 1% of the time
where the time goes in v1:
time: 53.7 us; the launch traced here: 53.5 us
  Pallas kernels  50.6 us (94%)
  between operations  1.95 us (4%)
  local copies, waits for them, and re-layouts  0.97 us (2%)
    pallas_call x1, Pallas kernels, body(): pl.pallas_call(functools.partial(kernel, n), out_shape=pltpu.VMEM(queries...  50.6 us

profile of v1, /device:TPU:0, one launch (start us, length us, event | category | flops | bytes accessed | tf_op | source)
XLA Modules:
  0.0 53.5 jit_solution(14685864153101584119)
XLA Ops:
  1.9 50.6 %windowed.1 = bf16[128,4096]{1,0:T(8,128)(2,1)S(1)} custom-call(s32[1]{0:T(128)S(6)} %copy.11.start_hbm, s32[1]{0:T(128)S(6)} %copy.12.length_hbm, s32[1]{0:T(128)S(6)} %copy.13.window_hbm, bf16[128,4096]{1,0:T(8,128)(2,1)} %q_hbm.1, bf16[128,1024]{1,0:T(8,128)(2,1)} %sk_hbm.1, bf16[128,1024]{1,0:T(8,128)(2,1)} %sv_hbm.1, bf16[2048,1024]{1,0:T(8,128)(2,1)} %ck_hbm.1, ...), custom_call_target="tpu_custom_call" | custom-call | flops 9126805504 | bytes 8912896 | tf_op jit(solution)/shard_map/windowed/pallas_call | solution.py:365
  52.5 1.0 %copy.10 = bf16[128,4096]{1,0:T(8,128)(2,1)} copy(bf16[128,4096]{1,0:T(8,128)(2,1)S(1)} %windowed.1) | data formatting | bytes 2097152

commit v2 on v1

--- a/solution.py
+++ b/solution.py
@@ -24,11 +24,11 @@
 
 
 def q_plan(heads):
-    return grouped([1, heads // 2 - 1, heads - heads // 2])
+    return grouped([1, 1, heads // 4, heads - heads // 4 - 2])
 
 
 def o_plan(heads):
-    return grouped([2] * ((heads - 2) // 2) + [1] * (heads - 2 * ((heads - 2) // 2)))
+    return grouped([2] * (heads // 4) + [1] * (heads - 2 * (heads // 4)))
 
 
 def l_plan(tiles):
@@ -37,18 +37,14 @@
 
 def kernel(
     n,
-    start_hbm,
-    length_hbm,
-    window_hbm,
+    words_own,
     q_hbm,
     sk_hbm,
     sv_hbm,
     ck_hbm,
     cv_hbm,
     out_ref,
-    start_ref,
-    length_ref,
-    window_ref,
+    words_got,
     q_own,
     q_got,
     keys,
@@ -63,7 +59,8 @@
     got_l,
     load_sem,
     own_sem,
-    word_sem,
+    ws_sem,
+    wr_sem,
     qs_sem,
     qr_sem,
     os_sem,
@@ -146,12 +143,15 @@
         pl.semaphore_signal(
             barrier, inc=1, device_id={"seq": lax.rem(me + d, n)}, device_id_type=MESH
         )
-    words = [
-        pltpu.make_async_copy(src, dst, word_sem.at[i])
-        for i, (src, dst) in enumerate(
-            ((start_hbm, start_ref), (length_hbm, length_ref), (window_hbm, window_ref))
-        )
-    ]
+    def tell(d):
+        return pltpu.make_async_remote_copy(
+            src_ref=words_own,
+            dst_ref=words_got,
+            send_sem=ws_sem.at[d - 1],
+            recv_sem=wr_sem.at[0],
+            device_id={"seq": lax.rem(me + d, n)},
+            device_id_type=MESH,
+        )
 
     def own_copy(h):
         return pltpu.make_async_copy(q_hbm.at[:, q_cols(h)], q_own.at[h], own_sem.at[h])
@@ -162,6 +162,12 @@
         pl.semaphore_wait(barrier, n - 1)
     for h in range(asks[0][1]):
         own_copy(h).wait()
+
+    @pl.when(me == 0)
+    def _():
+        for d in range(1, n):
+            tell(d).start()
+
     for d in range(1, n):
         ask(d, 0).start()
 
@@ -169,8 +175,6 @@
     def _(h):
         own_copy(h).start()
 
-    for copy in words:
-        copy.start()
     for copy in loads(0):
         copy.start()
     for i in range(1, len(asks)):
@@ -187,11 +191,23 @@
         for copy in loads(h):
             copy.start()
 
-    for copy in words:
-        copy.wait()
-    start = start_ref[0]
-    length = length_ref[0]
-    window = window_ref[0]
+    if n > 1:
+
+        @pl.when(me == 0)
+        def _():
+            words_got[...] = words_own[...]
+
+        @pl.when(me > 0)
+        def _():
+            tell(1).wait_recv()
+
+        words = words_got[...]
+    else:
+        words = words_own[...]
+    start, length, window = [
+        jnp.concatenate([words[i : i + 1, :]] * (rows // words.shape[1]), axis=1)
+        for i in range(3)
+    ]
     for d in range(n):
         source = lax.rem(me + n - d, n)
         q_pos = start + source * rows + lax.broadcasted_iota(jnp.int32, (1, rows), 1)
@@ -317,6 +333,11 @@
                 cols = pl.ds(pl.multiple_of((h * groups + g) * HD, HD), HD)
                 out_ref[:, cols] = o.T.astype(jnp.bfloat16)
 
+    @pl.when(me == 0)
+    def _():
+        for d in range(1, n):
+            tell(d).wait_send()
+
     for d in range(1, n):
         for i in range(len(asks)):
             ask(d, i).wait_send()
@@ -326,7 +347,20 @@
             answer_l(d, i).wait_send()
 
 
+def tile_of(start, length, window):
+    row = lax.broadcasted_iota(jnp.int32, (8, 128), 0)
+    return jnp.where(row == 0, start[0], jnp.where(row == 1, length[0], window[0]))
+
+
 def body(n, queries, span_keys, span_values, cache_keys, cache_values, start, length, window):
+    words = lax.cond(
+        lax.axis_index("seq") == 0,
+        tile_of,
+        lambda *_: jnp.zeros((8, 128), jnp.int32),
+        start,
+        length,
+        window,
+    )
     rows = queries.shape[0]
     cached = cache_keys.shape[0]
     span = span_keys.shape[0]
@@ -337,9 +371,7 @@
     peers = max(n - 1, 1)
     flops = 4 * n * queries.shape[1] * rows * total
     scratch = [
-        pltpu.SMEM((1,), jnp.int32),
-        pltpu.SMEM((1,), jnp.int32),
-        pltpu.SMEM((1,), jnp.int32),
+        pltpu.VMEM((8, 128), jnp.int32),
         pltpu.VMEM((heads, rows, groups * HD), jnp.bfloat16),
         pltpu.VMEM((peers, heads, rows, groups * HD), jnp.bfloat16),
         pltpu.VMEM((heads, total, HD), jnp.bfloat16),
@@ -354,7 +386,8 @@
         pltpu.VMEM((peers, heads * groups // 8, 8, rows), jnp.float32),
         pltpu.SemaphoreType.DMA((heads, 4)),
         pltpu.SemaphoreType.DMA((heads,)),
-        pltpu.SemaphoreType.DMA((3,)),
+        pltpu.SemaphoreType.DMA((peers,)),
+        pltpu.SemaphoreType.DMA((1,)),
         pltpu.SemaphoreType.DMA((peers, len(q_plan(heads)))),
         pltpu.SemaphoreType.DMA((peers, len(q_plan(heads)))),
         pltpu.SemaphoreType.DMA((peers, len(o_plan(heads)))),
@@ -365,7 +398,8 @@
     return pl.pallas_call(
         functools.partial(kernel, n),
         out_shape=pltpu.VMEM(queries.shape, jnp.bfloat16),
-        in_specs=[pl.BlockSpec(memory_space=pltpu.HBM)] * 8,
+        in_specs=[pl.BlockSpec(memory_space=pltpu.VMEM)]
+        + [pl.BlockSpec(memory_space=pltpu.HBM)] * 5,
         out_specs=pl.BlockSpec(memory_space=pltpu.VMEM),
         scratch_shapes=scratch,
         compiler_params=pltpu.CompilerParams(
@@ -375,7 +409,7 @@
             flops=flops, bytes_accessed=4 * total * HD * heads, transcendentals=flops // (4 * HD)
         ),
         name="windowed",
-    )(start, length, window, queries, span_keys, span_values, cache_keys, cache_values)
+    )(words, queries, span_keys, span_values, cache_keys, cache_values)
 
 
 def solution(mesh):

time: 53.7 us -> 52.3 us (0.974)
  other arithmetic: 0 us -> 2.02 us
  between operations: 1.95 us -> 0.01 us
  Pallas kernels: 50.6 us -> 49.1 us
    select_n x0 -> x2, other arithmetic: none -> 2.01 us  [the longest x1 1.29 us: tile_of(): jnp.where(row == 1, length[0], window[0])]
    pallas_call x1, Pallas kernels: 50.6 us -> 49.1 us  [body(): pl.pallas_call(functools.partial(kernel, n), out_shape=pltpu.VMEM(queries...]
where the time goes in v2:
time: 52.3 us; the launch traced here: 52.1 us
  Pallas kernels  49.1 us (94%)
  other arithmetic  2.02 us (4%)
  local copies, waits for them, and re-layouts  0.97 us (2%)
    pallas_call x1, Pallas kernels, body(): pl.pallas_call(functools.partial(kernel, n), out_shape=pltpu.VMEM(queries...  49.1 us
    select_n x1, other arithmetic, tile_of(): jnp.where(row == 1, length[0], window[0])  1.29 us

profile of v2, /device:TPU:0, one launch (start us, length us, event | category | flops | bytes accessed | tf_op | source)
XLA Modules:
  0.0 52.1 jit_solution(2746052475044046912)
XLA Ops:
  0.0 2.0 %conditional.1 = (s32[8,128]{1,0:T(8,128)S(1)}) conditional(s32[]{:T(128)} %convert_element_type.3, () %tuple.11, (s32[1]{0:T(128)}, s32[1]{0:T(128)}, s32[1]{0:T(128)}) %tuple.12), branch_computations={%region_0.0_spmd, %region_1.2_spmd} | conditional | flops 1048 | bytes 4196 | solution.py:356
  0.0 1.3 %compare_select_fusion = s32[8]{0:T(128)S(1)} fusion(s32[]{:T(128)} %bitcast.2, s32[]{:T(128)} %bitcast.1), kind=kLoop, calls=%fused_computation.1 | loop fusion | flops 16 | bytes 40 | tf_op jit(solution)/shard_map/cond/branch_1_fun/jit(_where)/select_n | solution.py:352
  1.3 0.7 %broadcast_select_fusion = s32[8,128]{1,0:T(8,128)S(1)} fusion(s32[8]{0:T(128)S(1)} %compare_select_fusion, s32[]{:T(128)} %bitcast, pred[8]{0:T(512)(128)(4,1)S(1)} %iota_compare_fusion), kind=kLoop, calls=%fused_computation | loop fusion | flops 1024 | bytes 4140 | tf_op jit(solution)/shard_map/cond/branch_1_fun/jit(_where)/select_n | solution.py:352
  2.0 49.1 %windowed.1 = bf16[128,4096]{1,0:T(8,128)(2,1)S(1)} custom-call(s32[8,128]{1,0:T(8,128)S(1)} %get-tuple-element.23.words_own, bf16[128,4096]{1,0:T(8,128)(2,1)} %q_hbm.1, bf16[128,1024]{1,0:T(8,128)(2,1)} %sk_hbm.1, bf16[128,1024]{1,0:T(8,128)(2,1)} %sv_hbm.1, bf16[2048,1024]{1,0:T(8,128)(2,1)} %ck_hbm.1, bf16[2048,1024]{1,0:T(8,128)(2,1)} %cv_hbm.1), custom_call_target="tpu_custom_call" | custom-call | flops 9126805504 | bytes 8912896 | tf_op jit(solution)/shard_map/windowed/pallas_call | solution.py:398
  51.2 1.0 %copy.15 = bf16[128,4096]{1,0:T(8,128)(2,1)} copy(bf16[128,4096]{1,0:T(8,128)(2,1)S(1)} %windowed.1) | data formatting | bytes 2097152
  (1 shorter events, 0.0 us)

commit v3 on v2

--- a/solution.py
+++ b/solution.py
@@ -116,6 +116,19 @@
             device_id_type=MESH,
         )
 
+    cut = HD * 3 // 8
+
+    def answer_last(d, part):
+        across = pl.ds(0, cut) if part == 0 else pl.ds(cut, HD - cut)
+        return pltpu.make_async_remote_copy(
+            src_ref=put_o.at[d - 1, heads - 1, across],
+            dst_ref=got_o.at[d - 1, heads - 1, across],
+            send_sem=os_sem.at[d - 1, len(answers) - 1 + part],
+            recv_sem=or_sem.at[d - 1, len(answers) - 1 + part],
+            device_id={"seq": lax.rem(me + n - d, n)},
+            device_id_type=MESH,
+        )
+
     def answer(d, i):
         across = pl.ds(answers[i][0], answers[i][1] - answers[i][0])
         return pltpu.make_async_remote_copy(
@@ -305,8 +318,15 @@
                 for d in range(1, n):
                     answer_l(d, i).start()
 
+    core = lax.rem(lax.axis_index("batch"), 2)
+
     for d in range(1, n):
-        answer(d, len(answers) - 1).start()
+        answer_last(d, 0).start()
+
+    @pl.when(core == 0)
+    def _():
+        for d in range(1, n):
+            answer_last(d, 1).start()
 
     for i, (first, last) in enumerate(answers):
         for t, (at, _) in enumerate(tallies):
@@ -314,7 +334,17 @@
                 for d in range(1, n):
                     answer_l(d, t).wait_recv()
         for d in range(1, n):
-            answer(d, i).wait_recv()
+            if i < len(answers) - 1:
+                answer(d, i).wait_recv()
+            else:
+                answer_last(d, 0).wait_recv()
+                answer_last(d, 1).wait_recv()
+        if i == len(answers) - 2:
+
+            @pl.when(core == 1)
+            def _():
+                for d in range(1, n):
+                    answer_last(d, 1).start()
 
         @pl.loop(first, last)
         def _(h):
@@ -341,8 +371,10 @@
     for d in range(1, n):
         for i in range(len(asks)):
             ask(d, i).wait_send()
-        for i in range(len(answers)):
+        for i in range(len(answers) - 1):
             answer(d, i).wait_send()
+        for part in range(2):
+            answer_last(d, part).wait_send()
         for i in range(len(tallies)):
             answer_l(d, i).wait_send()
 
@@ -390,8 +422,8 @@
         pltpu.SemaphoreType.DMA((1,)),
         pltpu.SemaphoreType.DMA((peers, len(q_plan(heads)))),
         pltpu.SemaphoreType.DMA((peers, len(q_plan(heads)))),
-        pltpu.SemaphoreType.DMA((peers, len(o_plan(heads)))),
-        pltpu.SemaphoreType.DMA((peers, len(o_plan(heads)))),
+        pltpu.SemaphoreType.DMA((peers, len(o_plan(heads)) + 1)),
+        pltpu.SemaphoreType.DMA((peers, len(o_plan(heads)) + 1)),
         pltpu.SemaphoreType.DMA((peers, len(l_plan(heads * groups // 8)))),
         pltpu.SemaphoreType.DMA((peers, len(l_plan(heads * groups // 8)))),
     ]

time: 52.3 us -> 51.7 us (0.989)
  Pallas kernels: 49.1 us -> 48.3 us
    pallas_call x1, Pallas kernels: 49.1 us -> 48.3 us  [body(): pl.pallas_call(functools.partial(kernel, n), out_shape=pltpu.VMEM(queries...]
where the time goes in v3:
time: 51.7 us; the launch traced here: 51.3 us
  Pallas kernels  48.3 us (93%)
  other arithmetic  2.02 us (4%)
  local copies, waits for them, and re-layouts  0.97 us (2%)
    pallas_call x1, Pallas kernels, body(): pl.pallas_call(functools.partial(kernel, n), out_shape=pltpu.VMEM(queries...  48.3 us
    select_n x1, other arithmetic, tile_of(): jnp.where(row == 1, length[0], window[0])  1.29 us

profile of v3, /device:TPU:0, one launch (start us, length us, event | category | flops | bytes accessed | tf_op | source)
XLA Modules:
  0.0 51.3 jit_solution(11262978235809863344)
XLA Ops:
  0.0 2.0 %conditional.1 = (s32[8,128]{1,0:T(8,128)S(1)}) conditional(s32[]{:T(128)} %convert_element_type.3, () %tuple.11, (s32[1]{0:T(128)}, s32[1]{0:T(128)}, s32[1]{0:T(128)}) %tuple.12), branch_computations={%region_0.0_spmd, %region_1.2_spmd} | conditional | flops 1048 | bytes 4196 | solution.py:388
  0.0 1.3 %compare_select_fusion = s32[8]{0:T(128)S(1)} fusion(s32[]{:T(128)} %bitcast.2, s32[]{:T(128)} %bitcast.1), kind=kLoop, calls=%fused_computation.1 | loop fusion | flops 16 | bytes 40 | tf_op jit(solution)/shard_map/cond/branch_1_fun/jit(_where)/select_n | solution.py:384
  1.3 0.7 %broadcast_select_fusion = s32[8,128]{1,0:T(8,128)S(1)} fusion(s32[8]{0:T(128)S(1)} %compare_select_fusion, s32[]{:T(128)} %bitcast, pred[8]{0:T(512)(128)(4,1)S(1)} %iota_compare_fusion), kind=kLoop, calls=%fused_computation | loop fusion | flops 1024 | bytes 4140 | tf_op jit(solution)/shard_map/cond/branch_1_fun/jit(_where)/select_n | solution.py:384
  2.0 48.3 %windowed.1 = bf16[128,4096]{1,0:T(8,128)(2,1)S(1)} custom-call(s32[8,128]{1,0:T(8,128)S(1)} %get-tuple-element.23.words_own, bf16[128,4096]{1,0:T(8,128)(2,1)} %q_hbm.1, bf16[128,1024]{1,0:T(8,128)(2,1)} %sk_hbm.1, bf16[128,1024]{1,0:T(8,128)(2,1)} %sv_hbm.1, bf16[2048,1024]{1,0:T(8,128)(2,1)} %ck_hbm.1, bf16[2048,1024]{1,0:T(8,128)(2,1)} %cv_hbm.1), custom_call_target="tpu_custom_call" | custom-call | flops 9126805504 | bytes 8912896 | tf_op jit(solution)/shard_map/windowed/pallas_call | solution.py:430
  50.3 1.0 %copy.15 = bf16[128,4096]{1,0:T(8,128)(2,1)} copy(bf16[128,4096]{1,0:T(8,128)(2,1)S(1)} %windowed.1) | data formatting | bytes 2097152
  (1 shorter events, 0.0 us)

commit v4 on v3

--- a/solution.py
+++ b/solution.py
@@ -116,7 +116,7 @@
             device_id_type=MESH,
         )
 
-    cut = HD * 3 // 8
+    cut = HD // 4
 
     def answer_last(d, part):
         across = pl.ds(0, cut) if part == 0 else pl.ds(cut, HD - cut)

time: 51.7 us -> 51.9 us (level)
  no operation moved by 1% of the time
where the time goes in v4:
time: 51.9 us; the launch traced here: 51.1 us
  Pallas kernels  48.1 us (93%)
  other arithmetic  2.02 us (4%)
  local copies, waits for them, and re-layouts  0.97 us (2%)
    pallas_call x1, Pallas kernels, body(): pl.pallas_call(functools.partial(kernel, n), out_shape=pltpu.VMEM(queries...  48.1 us
    select_n x1, other arithmetic, tile_of(): jnp.where(row == 1, length[0], window[0])  1.29 us

profile of v4, /device:TPU:0, one launch (start us, length us, event | category | flops | bytes accessed | tf_op | source)
XLA Modules:
  0.0 51.1 jit_solution(7433646554552268402)
XLA Ops:
  0.0 2.0 %conditional.1 = (s32[8,128]{1,0:T(8,128)S(1)}) conditional(s32[]{:T(128)} %convert_element_type.3, () %tuple.11, (s32[1]{0:T(128)}, s32[1]{0:T(128)}, s32[1]{0:T(128)}) %tuple.12), branch_computations={%region_0.0_spmd, %region_1.2_spmd} | conditional | flops 1048 | bytes 4196 | solution.py:388
  0.0 1.3 %compare_select_fusion = s32[8]{0:T(128)S(1)} fusion(s32[]{:T(128)} %bitcast.2, s32[]{:T(128)} %bitcast.1), kind=kLoop, calls=%fused_computation.1 | loop fusion | flops 16 | bytes 40 | tf_op jit(solution)/shard_map/cond/branch_1_fun/jit(_where)/select_n | solution.py:384
  1.3 0.7 %broadcast_select_fusion = s32[8,128]{1,0:T(8,128)S(1)} fusion(s32[8]{0:T(128)S(1)} %compare_select_fusion, s32[]{:T(128)} %bitcast, pred[8]{0:T(512)(128)(4,1)S(1)} %iota_compare_fusion), kind=kLoop, calls=%fused_computation | loop fusion | flops 1024 | bytes 4140 | tf_op jit(solution)/shard_map/cond/branch_1_fun/jit(_where)/select_n | solution.py:384
  2.0 48.1 %windowed.1 = bf16[128,4096]{1,0:T(8,128)(2,1)S(1)} custom-call(s32[8,128]{1,0:T(8,128)S(1)} %get-tuple-element.23.words_own, bf16[128,4096]{1,0:T(8,128)(2,1)} %q_hbm.1, bf16[128,1024]{1,0:T(8,128)(2,1)} %sk_hbm.1, bf16[128,1024]{1,0:T(8,128)(2,1)} %sv_hbm.1, bf16[2048,1024]{1,0:T(8,128)(2,1)} %ck_hbm.1, bf16[2048,1024]{1,0:T(8,128)(2,1)} %cv_hbm.1), custom_call_target="tpu_custom_call" | custom-call | flops 9126805504 | bytes 8912896 | tf_op jit(solution)/shard_map/windowed/pallas_call | solution.py:430
  50.1 1.0 %copy.15 = bf16[128,4096]{1,0:T(8,128)(2,1)} copy(bf16[128,4096]{1,0:T(8,128)(2,1)S(1)} %windowed.1) | data formatting | bytes 2097152
  (1 shorter events, 0.0 us)
